TPU v7x, 512 devices: a whole 4x4x16 slice. The times are simulated.
512 devices in a mesh: row: 64 (over z, x), col: 8 (over y, core).
Axes of the slice: x: 4, y: 4, z: 16, core: 2. Of those that a mesh axis runs over, the one named last changes fastest.
Arguments:
- gate_up: bfloat16 [4, 2, 14336, 4096], P(None, None, 'row', 'col'), may hold values from -0.09375 to 0.09375
- down_weight: bfloat16 [4, 4096, 14336], P(None, 'row', 'col'), may hold values from -0.046875 to 0.046875
- query_output: bfloat16 [4, 2, 4096, 4096], P(None, None, 'row', 'col'), may hold values from -0.09375 to 0.09375
- probe_gate: bfloat16 [4, 2, 16, 4096], P(None, None, None, 'col'), may hold values from -6 to 6
- probe_down: bfloat16 [4, 16, 14336], P(None, None, 'col'), may hold values from -6 to 6
- probe_query: bfloat16 [4, 2, 16, 4096], P(None, None, None, 'col'), may hold values from -6 to 6
Outputs:
- vector_gate: float32 [4, 2, 16, 4096], P(None, None, None, 'col')
- vector_down: float32 [4, 16, 14336], P(None, None, 'col')
- vector_query: float32 [4, 2, 16, 4096], P(None, None, None, 'col')
- sigma_gate: float32 [4, 2, 16], replicated
- sigma_down: float32 [4, 16], replicated
- sigma_query: float32 [4, 2, 16], replicated
All inputs are finite; a program needn't handle non-finite values.
Results may differ from a plain program's by a relative error of at most 0.0033.
Values may be sent and summed in bfloat16 or wider, within the bound.
No kernel may reach another device: no remote copies, remote signals or barrier semaphores. Data moves between devices by JAX's collectives and lax.ppermute only.
A program may use at most 64 MiB of HBM per device.

v0:
```python
import jax
import jax.numpy as jnp
from jax import lax
from jax.sharding import Mesh
from jax.sharding import PartitionSpec as P

ITERS = 2
ROW = ("row_0", "row_1")
epsilon = 1e-06


def copy_for_each(shard, axis):
    length = lax.axis_size(axis)
    return lax.all_to_all(
        jnp.broadcast_to(shard[None], (length, *shard.shape)), axis, 0, 0, tiled=True
    )


def of_everyone(shard, axis):
    everything = copy_for_each(shard, axis)
    return jnp.sum(everything, axis=0)


def over_axes(shard, axes):
    for axis in axes:
        shard = lax.psum(shard, axis)
    return shard


def body(gate_up, down_weight, query_output, probe_gate, probe_down, probe_query):
    row_count = lax.axis_size(ROW)
    col_count = lax.axis_size("col")
    weights = (gate_up, down_weight[:, None], query_output)
    vectors = (probe_gate, probe_down[:, None], probe_query)
    scaled_right = vectors
    spectral = None

    def left_factor(total, weight):
        return lax.rsqrt(total[..., None] / (weight.shape[2] * row_count) + epsilon)

    for turn in range(ITERS):
        partial_value = tuple(
            (
                jnp.einsum("lmoi,lmki->lmko", weight, vector, preferred_element_type=jnp.float32)
                for weight, vector in zip(weights, vectors)
            )
        )
        summed = jax.tree.map(lambda part: of_everyone(part, "col"), partial_value)
        squares = tuple((jnp.sum(piece * piece, axis=3) for piece in summed))
        totals = jax.tree.map(lambda part: over_axes(part, ROW), squares)
        left_vecs = tuple((piece.astype(jnp.bfloat16) for piece in summed))
        right_partial = tuple(
            (
                jnp.einsum("lmoi,lmko->lmki", weight, left, preferred_element_type=jnp.float32)
                for weight, left in zip(weights, left_vecs)
            )
        )
        raw_sums = lax.psum(right_partial, ROW)
        right_sums = tuple(
            (
                raw * left_factor(total, weight)
                for raw, total, weight in zip(raw_sums, totals, weights)
            )
        )
        right_squares = tuple((jnp.sum(piece * piece, axis=3) for piece in right_sums))
        right_totals = jax.tree.map(lambda part: of_everyone(part, "col"), right_squares)
        scaled_right = tuple(
            (
                piece * lax.rsqrt(total[..., None] / (piece.shape[3] * col_count) + epsilon)
                for piece, total in zip(right_sums, right_totals)
            )
        )
        spectral = tuple(
            (
                jnp.sqrt(total / (weight.shape[2] * row_count))
                for weight, total in zip(weights, right_totals)
            )
        )
        vectors = tuple((piece.astype(jnp.bfloat16) for piece in scaled_right))
    return (
        scaled_right[0],
        scaled_right[1][:, 0],
        scaled_right[2],
        spectral[0],
        spectral[1][:, 0],
        spectral[2],
    )


def solution(mesh):
    finer = Mesh(mesh.devices.reshape(16, 4, mesh.shape["col"]), ("row_0", "row_1", "col"))
    in_specs = (
        P(None, None, ROW, "col"),
        P(None, ROW, "col"),
        P(None, None, ROW, "col"),
        P(None, None, None, "col"),
        P(None, None, "col"),
        P(None, None, None, "col"),
    )
    out_specs = (
        P(None, None, None, "col"),
        P(None, None, "col"),
        P(None, None, None, "col"),
        P(),
        P(),
        P(),
    )
    return jax.shard_map(body, mesh=finer, in_specs=in_specs, out_specs=out_specs, check_vma=False)
```

profile of v0, /device:TPU:1, one launch (start us, length us, event | category | flops | bytes accessed | tf_op | source)
XLA Modules:
  0.0 717.1 jit_solution(13803138326627123436)
XLA Ops:
  7.2 1.8 fusion.22
  9.9 10.1 %all-to-all-start.4 = ((f32[8,1,4096]{2,1,0:T(1,128)}), f32[8,1,4096]{2,1,0:T(1,128)S(1)}, u32[]{:S(2)}, u32[]{:S(2)}) async-start(f32[8,1,4096]{2,1,0:T(1,128)} %reshape.197), calls=%async_computation.4 | async-start | bytes 262144 | tf_op jit(solution)/shard_map/all_to_all | solution.py:14
  20.3 1.0 reshape.201
  21.3 3.9 all-to-all-done.4
  25.2 4.2 all-to-all-start.8
  29.4 1.2 fusion.21
  30.7 5.2 all-to-all-done.8
  35.9 2.2 broadcast_in_dim.24
  38.1 5.1 all-to-all-start
  43.7 2.4 reduce.10
  46.2 1.7 reshape.198
  47.9 1.6 reduce_sum.228
  49.4 1.8 convolution_bitcast_fusion.1
  51.2 2.1 reduce.11
  53.3 1.0 reshape.202
  54.4 1.1 reduce_sum.238
  55.5 0.9 fusion.17
  56.4 2.0 all-to-all-done
  58.3 1.3 reduce_sum.220
  59.7 1.1 fusion.13
  61.1 45.7 %all-reduce.3 = (f32[4,2,16]{2,1,0:T(2,128)S(1)}, f32[4,1,16]{2,0,1:T(4,128)S(1)}, f32[4,2,16]{2,1,0:T(2,128)S(1)}) all-reduce(f32[4,2,16]{2,1,0:T(2,128)S(1)} %multiply_reduce_fusion.7, f32[4,1,16]{2,0,1:T(4,128)S(1)} %bitcast.30, f32[4,2,16]{2,1,0:T(2,128)S(1)} %multiply_reduce_fusion.9), channel_id=1, replica_groups=mesh['row_0'=16,'row_1'=4,'col'=8] {'row_0'}, use_global_device_ids=true, to_apply=%region_3.0 | all-reduce | flops 320 | bytes 2560 | tf_op jit(solution)/shard_map/psum | solution.py:26
  106.7 13.6 %all-reduce.5 = (f32[4,2,16]{2,1,0:T(2,128)S(1)}, f32[4,1,16]{2,0,1:T(4,128)S(1)}, f32[4,2,16]{2,1,0:T(2,128)S(1)}) all-reduce(f32[4,2,16]{2,1,0:T(2,128)S(1)} %get-tuple-element.15, f32[4,1,16]{2,0,1:T(4,128)S(1)} %get-tuple-element.16, f32[4,2,16]{2,1,0:T(2,128)S(1)} %get-tuple-element.17), channel_id=1, replica_groups=mesh['row_0'=16,'row_1'=4,'col'=8] {'row_1'}, use_global_device_ids=true, to_apply=%region_4.0 | all-reduce | flops 320 | bytes 2560 | tf_op jit(solution)/shard_map/psum | solution.py:26
  120.3 203.2 %all-reduce.11.cloned.1.call-done = (f32[4,2,16,512]{3,2,1,0:T(8,128)}, f32[4,1,16,1792]{3,2,0,1:T(8,128)}, f32[4,2,16,512]{3,2,1,0:T(8,128)}) async-done(((f32[4,2,16,512]{3,2,1,0:T(8,128)}, f32[4,1,16,1792]{3,2,0,1:T(8,128)}, f32[4,2,16,512]{3,2,1,0:T(8,128)}), (f32[4,2,16,512]{3,2,1,0:T(8,128)}, f32[4,1,16,1792]{3,2,0,1:T(8,128)}, f32[4,2,16,512]{3,2,1,0:T(8,128)})) %all-reduce.11.cloned.1.call-update) | async-done | bytes 983056 | tf_op jit(solution)/shard_map/psum | solution.py:58
  323.6 1.2 multiply_reduce_fusion.1
  325.4 15.1 %all-to-all-start.5 = ((f32[8,4,1,16]{3,2,1,0:T(1,128)}), f32[8,4,1,16]{3,2,1,0:T(1,128)S(1)}, u32[]{:S(2)}, u32[]{:S(2)}) async-start(f32[8,4,1,16]{3,2,1,0:T(1,128)} %broadcast_in_dim.29), calls=%async_computation.5 | async-start | bytes 32768 | tf_op jit(solution)/shard_map/all_to_all | solution.py:14
  340.5 1.1 multiply_reduce_fusion.3
  341.6 1.1 multiply_reduce_fusion.5
  344.2 1.0 all-to-all-done.5
  345.1 3.9 all-to-all-start.9
  349.1 1.4 fusion.1
  351.3 1.8 reshape.199
  354.2 4.3 all-to-all-start.1
  358.5 1.3 reduce.14
  361.3 1.2 fusion.6
  362.5 0.9 broadcast_in_dim.34
  363.4 2.1 reshape.205
  365.5 4.8 all-to-all-start.6
  372.4 3.3 all-to-all-done.6
  375.6 4.8 all-to-all-start.10
  380.4 1.3 fusion.5
  381.7 5.3 all-to-all-done.10
  387.0 2.1 broadcast_in_dim.26
  389.1 5.1 all-to-all-start.2
  394.2 2.4 reduce.13
  396.7 1.0 reshape.200
  398.3 1.8 convolution_bitcast_fusion
  400.1 2.1 reduce.15
  402.5 0.9 fusion.15
  403.4 6.0 all-to-all-done.2
  409.3 1.3 reduce_sum.224
  410.7 1.1 fusion.11
  412.1 41.4 %all-reduce.2 = (f32[4,2,16]{2,1,0:T(2,128)S(1)}, f32[4,1,16]{2,0,1:T(4,128)S(1)}, f32[4,2,16]{2,1,0:T(2,128)S(1)}) all-reduce(f32[4,2,16]{2,1,0:T(2,128)S(1)} %multiply_reduce_fusion.6, f32[4,1,16]{2,0,1:T(4,128)S(1)} %bitcast.31, f32[4,2,16]{2,1,0:T(2,128)S(1)} %multiply_reduce_fusion.8), channel_id=1, replica_groups=mesh['row_0'=16,'row_1'=4,'col'=8] {'row_0'}, use_global_device_ids=true, to_apply=%region_10.0 | all-reduce | flops 320 | bytes 2560 | tf_op jit(solution)/shard_map/psum | solution.py:26
  453.4 13.0 %all-reduce.4 = (f32[4,2,16]{2,1,0:T(2,128)S(1)}, f32[4,1,16]{2,0,1:T(4,128)S(1)}, f32[4,2,16]{2,1,0:T(2,128)S(1)}) all-reduce(f32[4,2,16]{2,1,0:T(2,128)S(1)} %get-tuple-element.12, f32[4,1,16]{2,0,1:T(4,128)S(1)} %get-tuple-element.13, f32[4,2,16]{2,1,0:T(2,128)S(1)} %get-tuple-element.14), channel_id=1, replica_groups=mesh['row_0'=16,'row_1'=4,'col'=8] {'row_1'}, use_global_device_ids=true, to_apply=%region_11.0 | all-reduce | flops 320 | bytes 2560 | tf_op jit(solution)/shard_map/psum | solution.py:26
  466.4 203.1 %all-reduce.9.cloned.1.call-done = (f32[4,2,16,512]{3,2,1,0:T(8,128)}, f32[4,1,16,1792]{3,2,0,1:T(8,128)}, f32[4,2,16,512]{3,2,1,0:T(8,128)}) async-done(((f32[4,2,16,512]{3,2,1,0:T(8,128)}, f32[4,1,16,1792]{3,2,0,1:T(8,128)}, f32[4,2,16,512]{3,2,1,0:T(8,128)}), (f32[4,2,16,512]{3,2,1,0:T(8,128)}, f32[4,1,16,1792]{3,2,0,1:T(8,128)}, f32[4,2,16,512]{3,2,1,0:T(8,128)})) %all-reduce.9.cloned.1.call-update) | async-done | bytes 983056 | tf_op jit(solution)/shard_map/psum | solution.py:58
  669.6 1.3 multiply_reduce_fusion
  671.5 15.1 %all-to-all-start.7 = ((f32[8,4,1,16]{3,2,1,0:T(1,128)}), f32[8,4,1,16]{3,2,1,0:T(1,128)S(1)}, u32[]{:S(2)}, u32[]{:S(2)}) async-start(f32[8,4,1,16]{3,2,1,0:T(1,128)} %broadcast_in_dim.31), calls=%async_computation.7 | async-start | bytes 32768 | tf_op jit(solution)/shard_map/all_to_all | solution.py:14
  686.5 1.1 multiply_reduce_fusion.2
  687.7 1.1 multiply_reduce_fusion.4
  690.2 1.0 all-to-all-done.7
  691.2 3.9 all-to-all-start.11
  695.7 1.9 multiply_bitcast_fusion
  697.6 2.0 all-to-all-done.11
  699.7 3.9 all-to-all-start.3
  705.7 2.4 all-to-all-done.3
  (83 shorter events, 17.7 us)
Async XLA Ops:
  7.2 22.3 %copy-start = (bf16[4,2,224,512]{3,2,1,0:T(8,128)(2,1)S(1)}, bf16[4,2,224,512]{3,2,1,0:T(8,128)(2,1)}, u32[]{:S(2)}) copy-start(bf16[4,2,224,512]{3,2,1,0:T(8,128)(2,1)} %param.6) | copy-start | bytes 5505028
  7.2 12.8 %copy-start.11 = (bf16[4,2,16,512]{3,2,1,0:T(8,128)(2,1)S(1)}, bf16[4,2,16,512]{3,2,1,0:T(8,128)(2,1)}, u32[]{:S(2)}) copy-start(bf16[4,2,16,512]{3,2,1,0:T(8,128)(2,1)} %param.11) | copy-start | bytes 393220
  7.2 12.8 %copy-start.2 = (bf16[4,2,64,512]{3,2,1,0:T(8,128)(2,1)S(1)}, bf16[4,2,64,512]{3,2,1,0:T(8,128)(2,1)}, u32[]{:S(2)}) copy-start(bf16[4,2,64,512]{3,2,1,0:T(8,128)(2,1)} %param.8) | copy-start | bytes 1572868
  9.0 20.4 %copy-start.10 = (bf16[4,2,16,512]{3,2,1,0:T(8,128)(2,1)S(1)}, bf16[4,2,16,512]{3,2,1,0:T(8,128)(2,1)}, u32[]{:S(2)}) copy-start(bf16[4,2,16,512]{3,2,1,0:T(8,128)(2,1)} %param.9) | copy-start | bytes 393220
  9.9 15.4 %all-to-all-start.4 = ((f32[8,1,4096]{2,1,0:T(1,128)}), f32[8,1,4096]{2,1,0:T(1,128)S(1)}, u32[]{:S(2)}, u32[]{:S(2)}) async-start(f32[8,1,4096]{2,1,0:T(1,128)} %reshape.197), calls=%async_computation.4 | async-start | bytes 262144 | tf_op jit(solution)/shard_map/all_to_all | solution.py:14
  25.2 4.2 copy-start.7
  25.2 10.7 %all-to-all-start.8 = ((f32[8,1,8192]{2,1,0:T(1,128)}), f32[8,1,8192]{2,1,0:T(1,128)S(1)}, u32[]{:S(2)}, u32[]{:S(2)}) async-start(f32[8,1,8192]{2,1,0:T(1,128)} %reshape.201), calls=%async_computation.8 | async-start | bytes 524288 | tf_op jit(solution)/shard_map/all_to_all | solution.py:14
  30.7 18.8 %copy-start.1 = (bf16[4,64,1792]{2,1,0:T(8,128)(2,1)S(1)}, bf16[4,64,1792]{2,1,0:T(8,128)(2,1)}, u32[]{:S(2)}) copy-start(bf16[4,64,1792]{2,1,0:T(8,128)(2,1)} %param.7) | copy-start | bytes 2752516
  35.9 12.0 %copy-start.4 = (f32[8,1,8192]{2,1,0:T(1,128)}, f32[8,1,8192]{2,1,0:T(1,128)S(1)}, u32[]{:S(2)}) copy-start(f32[8,1,8192]{2,1,0:T(1,128)S(1)} %all-to-all-done.8) | copy-start | bytes 786436
  38.1 20.2 %all-to-all-start = ((f32[8,4,2,16,224]{4,3,2,1,0:T(8,128)}), f32[8,4,2,16,224]{4,3,2,1,0:T(8,128)}, u32[]{:S(2)}, u32[]{:S(2)}) async-start(f32[8,4,2,16,224]{4,3,2,1,0:T(8,128)} %broadcast_in_dim.24), calls=%async_computation | async-start | bytes 2097152 | tf_op jit(solution)/shard_map/all_to_all | solution.py:14
  43.2 280.4 %all-reduce.11.cloned.1.call-start = ((), (), s32[]{:S(2)}) async-start(), calls=%async_computation.13 | async-start | bytes 1966080 | tf_op jit(solution)/shard_map/psum | solution.py:58
  59.7 1.1 copy-start.8
  325.4 19.7 %all-to-all-start.5 = ((f32[8,4,1,16]{3,2,1,0:T(1,128)}), f32[8,4,1,16]{3,2,1,0:T(1,128)S(1)}, u32[]{:S(2)}, u32[]{:S(2)}) async-start(f32[8,4,1,16]{3,2,1,0:T(1,128)} %broadcast_in_dim.29), calls=%async_computation.5 | async-start | bytes 32768 | tf_op jit(solution)/shard_map/all_to_all | solution.py:14
  345.1 8.5 %all-to-all-start.9 = ((f32[8,1,128]{2,1,0:T(1,128)}), f32[8,1,128]{2,1,0:T(1,128)S(1)}, u32[]{:S(2)}, u32[]{:S(2)}) async-start(f32[8,1,128]{2,1,0:T(1,128)} %reshape.203), calls=%async_computation.9 | async-start | bytes 8192 | tf_op jit(solution)/shard_map/all_to_all | solution.py:14
  351.3 29.1 %copy-start.3 = (f32[4,2,16,512]{3,2,1,0:T(8,128)S(1)}, f32[4,2,16,512]{3,2,1,0:T(8,128)}, u32[]{:S(2)}) copy-start(f32[4,2,16,512]{3,2,1,0:T(8,128)} %get-tuple-element.9) | copy-start | bytes 786436
  353.6 0.6 copy-start.12
  354.2 11.3 %all-to-all-start.1 = ((f32[8,1,128]{2,1,0:T(1,128)}), f32[8,1,128]{2,1,0:T(1,128)S(1)}, u32[]{:S(2)}, u32[]{:S(2)}) async-start(f32[8,1,128]{2,1,0:T(1,128)} %reshape.193), calls=%async_computation.1 | async-start | bytes 8192 | tf_op jit(solution)/shard_map/all_to_all | solution.py:14
  365.5 10.2 %all-to-all-start.6 = ((f32[8,1,4096]{2,1,0:T(1,128)}), f32[8,1,4096]{2,1,0:T(1,128)}, u32[]{:S(2)}, u32[]{:S(2)}) async-start(f32[8,1,4096]{2,1,0:T(1,128)} %reshape.199), calls=%async_computation.6 | async-start | bytes 262144 | tf_op jit(solution)/shard_map/all_to_all | solution.py:14
  375.6 11.4 %all-to-all-start.10 = ((f32[8,1,8192]{2,1,0:T(1,128)}), f32[8,1,8192]{2,1,0:T(1,128)}, u32[]{:S(2)}, u32[]{:S(2)}) async-start(f32[8,1,8192]{2,1,0:T(1,128)} %reshape.205), calls=%async_computation.10 | async-start | bytes 524288 | tf_op jit(solution)/shard_map/all_to_all | solution.py:14
  389.1 20.2 %all-to-all-start.2 = ((f32[8,4,2,16,224]{4,3,2,1,0:T(8,128)}), f32[8,4,2,16,224]{4,3,2,1,0:T(8,128)}, u32[]{:S(2)}, u32[]{:S(2)}) async-start(f32[8,4,2,16,224]{4,3,2,1,0:T(8,128)} %broadcast_in_dim.26), calls=%async_computation.2 | async-start | bytes 2097152 | tf_op jit(solution)/shard_map/all_to_all | solution.py:14
  394.2 275.3 %all-reduce.9.cloned.1.call-start = ((), (), s32[]{:S(2)}) async-start(), calls=%async_computation.12 | async-start | bytes 1966080 | tf_op jit(solution)/shard_map/psum | solution.py:58
  410.7 1.1 copy-start.9
  669.6 35.3 %copy-start.6 = (f32[4,2,16,512]{3,2,1,0:T(8,128)S(1)}, f32[4,2,16,512]{3,2,1,0:T(8,128)}, u32[]{:S(2)}) copy-start(f32[4,2,16,512]{3,2,1,0:T(8,128)} %get-tuple-element.8) | copy-start | bytes 786436
  669.6 39.9 %copy-start.5 = (f32[4,2,16,512]{3,2,1,0:T(8,128)S(1)}, f32[4,2,16,512]{3,2,1,0:T(8,128)}, u32[]{:S(2)}) copy-start(f32[4,2,16,512]{3,2,1,0:T(8,128)} %get-tuple-element.6) | copy-start | bytes 786436
  671.5 19.7 %all-to-all-start.7 = ((f32[8,4,1,16]{3,2,1,0:T(1,128)}), f32[8,4,1,16]{3,2,1,0:T(1,128)S(1)}, u32[]{:S(2)}, u32[]{:S(2)}) async-start(f32[8,4,1,16]{3,2,1,0:T(1,128)} %broadcast_in_dim.31), calls=%async_computation.7 | async-start | bytes 32768 | tf_op jit(solution)/shard_map/all_to_all | solution.py:14
  691.2 8.5 %all-to-all-start.11 = ((f32[8,1,128]{2,1,0:T(1,128)}), f32[8,1,128]{2,1,0:T(1,128)S(1)}, u32[]{:S(2)}, u32[]{:S(2)}) async-start(f32[8,1,128]{2,1,0:T(1,128)} %reshape.207), calls=%async_computation.11 | async-start | bytes 8192 | tf_op jit(solution)/shard_map/all_to_all | solution.py:14
  699.7 8.5 %all-to-all-start.3 = ((f32[8,1,128]{2,1,0:T(1,128)}), f32[8,1,128]{2,1,0:T(1,128)S(1)}, u32[]{:S(2)}, u32[]{:S(2)}) async-start(f32[8,1,128]{2,1,0:T(1,128)} %reshape.195), calls=%async_computation.3 | async-start | bytes 8192 | tf_op jit(solution)/shard_map/all_to_all | solution.py:14
Sparse Core Ops, SparseCore 0:
  60.9 262.6 all-reduce.10
  411.9 257.6 all-reduce.8
where the time goes:
time: 719 us; the launch traced here: 717 us
  waiting for transfers between devices  439 us (61%)
  blocking collectives  114 us (16%)
  starting transfers between devices  80.4 us (11%)
  other arithmetic  32.7 us (5%)
  local copies, waits for them, and re-layouts  22.5 us (3%)
  matrix products  14.6 us (2%)
  between operations  14.3 us (2%)
    psum x2, waiting for transfers between devices, body(): raw_sums = lax.psum(right_partial, ROW)  406 us
    psum x4, blocking collectives, over_axes(): shard = lax.psum(shard, axis)  114 us
    all_to_all x12, starting transfers between devices, copy_for_each(): lax.all_to_all(jnp.broadcast_to(shard[None], (length, *shard.shape)), axi...  80.4 us
    all_to_all x12, waiting for transfers between devices, copy_for_each(): lax.all_to_all(jnp.broadcast_to(shard[None], (length, *shard.shape)), axi...  32.5 us
    unnamed x42, local copies, waits for them, and re-layouts  14.8 us
  transfers between devices with their start and end apart: 14, of which 13 were waited for; matrix products, arithmetic and copies ran while one was open for 7% of the time, Pallas kernels for 0%

commit v1 on v0

--- a/solution.py
+++ b/solution.py
@@ -55,7 +55,7 @@
                 for weight, left in zip(weights, left_vecs)
             )
         )
-        raw_sums = lax.psum(right_partial, ROW)
+        raw_sums = lax.psum(lax.psum(right_partial, "row_0"), "row_1")
         right_sums = tuple(
             (
                 raw * left_factor(total, weight)

time: 719 us -> 592 us (0.82)
  waiting for transfers between devices: 439 us -> 308 us
  starting transfers between devices: 80.4 us -> 88.1 us
    psum x2 -> x4, waiting for transfers between devices: 406 us -> 275 us  [body(): raw_sums = lax.psum(lax.psum(right_partial, 'row_0'), 'row_1')]
    all_to_all x12, starting transfers between devices: 80.4 us -> 88 us  [copy_for_each(): lax.all_to_all(jnp.broadcast_to(shard[None], (length, *shard.shape)), axi...]
  transfers between devices with their start and end apart: 14 -> 16, of which waited for: 13 -> 15; matrix products, arithmetic and copies ran while one was open for 7% -> 9% of each run, Pallas kernels for 0% -> 0%
where the time goes in v1:
time: 592 us; the launch traced here: 590 us
  waiting for transfers between devices  308 us (52%)
  blocking collectives  110 us (19%)
  starting transfers between devices  88.1 us (15%)
  other arithmetic  32.7 us (6%)
  local copies, waits for them, and re-layouts  22.5 us (4%)
  matrix products  14.6 us (2%)
  between operations  14 us (2%)
    psum x4, waiting for transfers between devices, body(): raw_sums = lax.psum(lax.psum(right_partial, 'row_0'), 'row_1')  275 us
    psum x4, blocking collectives, over_axes(): shard = lax.psum(shard, axis)  110 us
    all_to_all x12, starting transfers between devices, copy_for_each(): lax.all_to_all(jnp.broadcast_to(shard[None], (length, *shard.shape)), axi...  88 us
    all_to_all x12, waiting for transfers between devices, copy_for_each(): lax.all_to_all(jnp.broadcast_to(shard[None], (length, *shard.shape)), axi...  32.5 us
    unnamed x42, local copies, waits for them, and re-layouts  14.8 us
    all_to_all x8, other arithmetic, copy_for_each(): lax.all_to_all(jnp.broadcast_to(shard[None], (length, *shard.shape)), axi...  12.1 us
  transfers between devices with their start and end apart: 16, of which 15 were waited for; matrix products, arithmetic and copies ran while one was open for 9% of the time, Pallas kernels for 0%

profile of v1, /device:TPU:1, one launch (start us, length us, event | category | flops | bytes accessed | tf_op | source)
XLA Modules:
  0.0 590.1 jit_solution(188110429424923371)
XLA Ops:
  7.2 1.8 fusion.22
  9.9 10.1 %all-to-all-start.4 = ((f32[8,1,4096]{2,1,0:T(1,128)}), f32[8,1,4096]{2,1,0:T(1,128)S(1)}, u32[]{:S(2)}, u32[]{:S(2)}) async-start(f32[8,1,4096]{2,1,0:T(1,128)} %reshape.197), calls=%async_computation.4 | async-start | bytes 262144 | tf_op jit(solution)/shard_map/all_to_all | solution.py:14
  20.3 1.0 reshape.201
  21.3 3.9 all-to-all-done.4
  25.2 4.2 all-to-all-start.8
  29.4 1.2 fusion.21
  30.7 5.2 all-to-all-done.8
  35.9 2.2 broadcast_in_dim.24
  38.1 5.1 all-to-all-start
  43.7 2.4 reduce.10
  46.2 1.7 reshape.198
  47.9 1.6 reduce_sum.228
  49.4 1.8 convolution_bitcast_fusion.1
  51.2 2.1 reduce.11
  53.3 1.0 reshape.202
  54.4 1.1 reduce_sum.238
  55.5 0.9 fusion.17
  56.4 2.0 all-to-all-done
  58.3 1.3 reduce_sum.220
  59.7 1.1 fusion.13
  60.8 128.9 %all-reduce.15.cloned.1.call-done = (f32[4,2,16,512]{3,2,1,0:T(8,128)}, f32[4,1,16,1792]{3,2,0,1:T(8,128)}, f32[4,2,16,512]{3,2,1,0:T(8,128)}) async-done(((f32[4,2,16,512]{3,2,1,0:T(8,128)}, f32[4,1,16,1792]{3,2,0,1:T(8,128)}, f32[4,2,16,512]{3,2,1,0:T(8,128)}), (f32[4,2,16,512]{3,2,1,0:T(8,128)}, f32[4,1,16,1792]{3,2,0,1:T(8,128)}, f32[4,2,16,512]{3,2,1,0:T(8,128)})) %all-reduce.15.cloned.1.call-update) | async-done | bytes 983056 | tf_op jit(solution)/shard_map/psum | solution.py:58
  190.1 41.3 %all-reduce.1 = (f32[4,2,16]{2,1,0:T(2,128)S(1)}, f32[4,1,16]{2,0,1:T(4,128)S(1)}, f32[4,2,16]{2,1,0:T(2,128)S(1)}) all-reduce(f32[4,2,16]{2,1,0:T(2,128)S(1)} %multiply_reduce_fusion.7, f32[4,1,16]{2,0,1:T(4,128)S(1)} %bitcast.30, f32[4,2,16]{2,1,0:T(2,128)S(1)} %multiply_reduce_fusion.9), channel_id=1, replica_groups=mesh['row_0'=16,'row_1'=4,'col'=8] {'row_0'}, use_global_device_ids=true, to_apply=%region_4.0 | all-reduce | flops 320 | bytes 2560 | tf_op jit(solution)/shard_map/psum | solution.py:26
  231.4 13.9 %all-reduce.5 = (f32[4,2,16]{2,1,0:T(2,128)S(1)}, f32[4,1,16]{2,0,1:T(4,128)S(1)}, f32[4,2,16]{2,1,0:T(2,128)S(1)}) all-reduce(f32[4,2,16]{2,1,0:T(2,128)S(1)} %get-tuple-element.9, f32[4,1,16]{2,0,1:T(4,128)S(1)} %get-tuple-element.10, f32[4,2,16]{2,1,0:T(2,128)S(1)} %get-tuple-element.11), channel_id=1, replica_groups=mesh['row_0'=16,'row_1'=4,'col'=8] {'row_1'}, use_global_device_ids=true, to_apply=%region_5.0 | all-reduce | flops 320 | bytes 2560 | tf_op jit(solution)/shard_map/psum | solution.py:26
  245.3 12.1 %all-reduce.19.cloned.1.call-done = (f32[4,2,16,512]{3,2,1,0:T(8,128)}, f32[4,1,16,1792]{3,2,0,1:T(8,128)}, f32[4,2,16,512]{3,2,1,0:T(8,128)}) async-done(((f32[4,2,16,512]{3,2,1,0:T(8,128)}, f32[4,1,16,1792]{3,2,0,1:T(8,128)}, f32[4,2,16,512]{3,2,1,0:T(8,128)}), (f32[4,2,16,512]{3,2,1,0:T(8,128)}, f32[4,1,16,1792]{3,2,0,1:T(8,128)}, f32[4,2,16,512]{3,2,1,0:T(8,128)})) %all-reduce.19.cloned.1.call-update) | async-done | bytes 983056 | tf_op jit(solution)/shard_map/psum | solution.py:58
  257.4 1.2 multiply_reduce_fusion.1
  259.2 18.8 %all-to-all-start.5 = ((f32[8,4,1,16]{3,2,1,0:T(1,128)}), f32[8,4,1,16]{3,2,1,0:T(1,128)S(1)}, u32[]{:S(2)}, u32[]{:S(2)}) async-start(f32[8,4,1,16]{3,2,1,0:T(1,128)} %broadcast_in_dim.29), calls=%async_computation.5 | async-start | bytes 32768 | tf_op jit(solution)/shard_map/all_to_all | solution.py:14
  278.0 1.1 multiply_reduce_fusion.3
  279.1 1.1 multiply_reduce_fusion.5
  281.7 1.0 all-to-all-done.5
  282.7 3.9 all-to-all-start.9
  286.6 1.4 fusion.1
  288.8 1.8 reshape.199
  291.7 4.3 all-to-all-start.1
  296.0 1.3 reduce.14
  298.8 1.2 fusion.6
  300.9 2.1 reshape.205
  303.0 4.8 all-to-all-start.6
  309.9 3.3 all-to-all-done.6
  313.2 4.8 all-to-all-start.10
  317.9 1.3 fusion.5
  319.2 5.3 all-to-all-done.10
  324.5 2.1 broadcast_in_dim.26
  326.6 5.1 all-to-all-start.2
  331.8 2.4 reduce.13
  334.2 1.0 reshape.200
  335.8 1.8 convolution_bitcast_fusion
  337.6 2.1 reduce.15
  340.9 6.0 %all-to-all-done.2 = f32[8,4,2,16,224]{4,3,2,1,0:T(8,128)} async-done(((f32[8,4,2,16,224]{4,3,2,1,0:T(8,128)}), f32[8,4,2,16,224]{4,3,2,1,0:T(8,128)}, u32[]{:S(2)}, u32[]{:S(2)}) %all-to-all-start.2) | async-done | bytes 917536 | tf_op jit(solution)/shard_map/all_to_all | solution.py:14
  346.9 1.3 reduce_sum.224
  348.2 1.1 fusion.11
  349.3 122.2 %all-reduce.13.cloned.1.call-done = (f32[4,2,16,512]{3,2,1,0:T(8,128)}, f32[4,1,16,1792]{3,2,0,1:T(8,128)}, f32[4,2,16,512]{3,2,1,0:T(8,128)}) async-done(((f32[4,2,16,512]{3,2,1,0:T(8,128)}, f32[4,1,16,1792]{3,2,0,1:T(8,128)}, f32[4,2,16,512]{3,2,1,0:T(8,128)}), (f32[4,2,16,512]{3,2,1,0:T(8,128)}, f32[4,1,16,1792]{3,2,0,1:T(8,128)}, f32[4,2,16,512]{3,2,1,0:T(8,128)})) %all-reduce.13.cloned.1.call-update) | async-done | bytes 983056 | tf_op jit(solution)/shard_map/psum | solution.py:58
  471.9 41.9 %all-reduce = (f32[4,2,16]{2,1,0:T(2,128)S(1)}, f32[4,1,16]{2,0,1:T(4,128)S(1)}, f32[4,2,16]{2,1,0:T(2,128)S(1)}) all-reduce(f32[4,2,16]{2,1,0:T(2,128)S(1)} %multiply_reduce_fusion.6, f32[4,1,16]{2,0,1:T(4,128)S(1)} %bitcast.31, f32[4,2,16]{2,1,0:T(2,128)S(1)} %multiply_reduce_fusion.8), channel_id=1, replica_groups=mesh['row_0'=16,'row_1'=4,'col'=8] {'row_0'}, use_global_device_ids=true, to_apply=%region_12.0 | all-reduce | flops 320 | bytes 2560 | tf_op jit(solution)/shard_map/psum | solution.py:26
  513.7 13.3 %all-reduce.4 = (f32[4,2,16]{2,1,0:T(2,128)S(1)}, f32[4,1,16]{2,0,1:T(4,128)S(1)}, f32[4,2,16]{2,1,0:T(2,128)S(1)}) all-reduce(f32[4,2,16]{2,1,0:T(2,128)S(1)} %get-tuple-element.6, f32[4,1,16]{2,0,1:T(4,128)S(1)} %get-tuple-element.7, f32[4,2,16]{2,1,0:T(2,128)S(1)} %get-tuple-element.8), channel_id=1, replica_groups=mesh['row_0'=16,'row_1'=4,'col'=8] {'row_1'}, use_global_device_ids=true, to_apply=%region_13.0 | all-reduce | flops 320 | bytes 2560 | tf_op jit(solution)/shard_map/psum | solution.py:26
  527.1 11.9 %all-reduce.17.cloned.1.call-done = (f32[4,2,16,512]{3,2,1,0:T(8,128)}, f32[4,1,16,1792]{3,2,0,1:T(8,128)}, f32[4,2,16,512]{3,2,1,0:T(8,128)}) async-done(((f32[4,2,16,512]{3,2,1,0:T(8,128)}, f32[4,1,16,1792]{3,2,0,1:T(8,128)}, f32[4,2,16,512]{3,2,1,0:T(8,128)}), (f32[4,2,16,512]{3,2,1,0:T(8,128)}, f32[4,1,16,1792]{3,2,0,1:T(8,128)}, f32[4,2,16,512]{3,2,1,0:T(8,128)})) %all-reduce.17.cloned.1.call-update) | async-done | bytes 983056 | tf_op jit(solution)/shard_map/psum | solution.py:58
  539.0 1.3 multiply_reduce_fusion
  540.9 19.0 %all-to-all-start.7 = ((f32[8,4,1,16]{3,2,1,0:T(1,128)}), f32[8,4,1,16]{3,2,1,0:T(1,128)S(1)}, u32[]{:S(2)}, u32[]{:S(2)}) async-start(f32[8,4,1,16]{3,2,1,0:T(1,128)} %broadcast_in_dim.31), calls=%async_computation.7 | async-start | bytes 32768 | tf_op jit(solution)/shard_map/all_to_all | solution.py:14
  559.9 1.1 multiply_reduce_fusion.2
  561.0 1.1 multiply_reduce_fusion.4
  563.6 1.0 all-to-all-done.7
  564.5 3.9 all-to-all-start.11
  569.1 1.9 multiply_bitcast_fusion
  571.0 2.0 all-to-all-done.11
  573.0 3.9 all-to-all-start.3
  579.0 2.4 all-to-all-done.3
  (89 shorter events, 19.6 us)
Async XLA Ops:
  7.2 22.3 %copy-start = (bf16[4,2,224,512]{3,2,1,0:T(8,128)(2,1)S(1)}, bf16[4,2,224,512]{3,2,1,0:T(8,128)(2,1)}, u32[]{:S(2)}) copy-start(bf16[4,2,224,512]{3,2,1,0:T(8,128)(2,1)} %param.6) | copy-start | bytes 5505028
  7.2 12.8 %copy-start.11 = (bf16[4,2,16,512]{3,2,1,0:T(8,128)(2,1)S(1)}, bf16[4,2,16,512]{3,2,1,0:T(8,128)(2,1)}, u32[]{:S(2)}) copy-start(bf16[4,2,16,512]{3,2,1,0:T(8,128)(2,1)} %param.11) | copy-start | bytes 393220
  7.2 12.8 %copy-start.2 = (bf16[4,2,64,512]{3,2,1,0:T(8,128)(2,1)S(1)}, bf16[4,2,64,512]{3,2,1,0:T(8,128)(2,1)}, u32[]{:S(2)}) copy-start(bf16[4,2,64,512]{3,2,1,0:T(8,128)(2,1)} %param.8) | copy-start | bytes 1572868
  9.0 20.4 %copy-start.10 = (bf16[4,2,16,512]{3,2,1,0:T(8,128)(2,1)S(1)}, bf16[4,2,16,512]{3,2,1,0:T(8,128)(2,1)}, u32[]{:S(2)}) copy-start(bf16[4,2,16,512]{3,2,1,0:T(8,128)(2,1)} %param.9) | copy-start | bytes 393220
  9.9 15.4 %all-to-all-start.4 = ((f32[8,1,4096]{2,1,0:T(1,128)}), f32[8,1,4096]{2,1,0:T(1,128)S(1)}, u32[]{:S(2)}, u32[]{:S(2)}) async-start(f32[8,1,4096]{2,1,0:T(1,128)} %reshape.197), calls=%async_computation.4 | async-start | bytes 262144 | tf_op jit(solution)/shard_map/all_to_all | solution.py:14
  25.2 4.2 copy-start.7
  25.2 10.7 %all-to-all-start.8 = ((f32[8,1,8192]{2,1,0:T(1,128)}), f32[8,1,8192]{2,1,0:T(1,128)S(1)}, u32[]{:S(2)}, u32[]{:S(2)}) async-start(f32[8,1,8192]{2,1,0:T(1,128)} %reshape.201), calls=%async_computation.8 | async-start | bytes 524288 | tf_op jit(solution)/shard_map/all_to_all | solution.py:14
  30.7 18.8 %copy-start.1 = (bf16[4,64,1792]{2,1,0:T(8,128)(2,1)S(1)}, bf16[4,64,1792]{2,1,0:T(8,128)(2,1)}, u32[]{:S(2)}) copy-start(bf16[4,64,1792]{2,1,0:T(8,128)(2,1)} %param.7) | copy-start | bytes 2752516
  35.9 12.0 %copy-start.4 = (f32[8,1,8192]{2,1,0:T(1,128)}, f32[8,1,8192]{2,1,0:T(1,128)S(1)}, u32[]{:S(2)}) copy-start(f32[8,1,8192]{2,1,0:T(1,128)S(1)} %all-to-all-done.8) | copy-start | bytes 786436
  38.1 20.2 %all-to-all-start = ((f32[8,4,2,16,224]{4,3,2,1,0:T(8,128)}), f32[8,4,2,16,224]{4,3,2,1,0:T(8,128)}, u32[]{:S(2)}, u32[]{:S(2)}) async-start(f32[8,4,2,16,224]{4,3,2,1,0:T(8,128)} %broadcast_in_dim.24), calls=%async_computation | async-start | bytes 2097152 | tf_op jit(solution)/shard_map/all_to_all | solution.py:14
  43.2 146.5 %all-reduce.15.cloned.1.call-start = ((), (), s32[]{:S(2)}) async-start(), calls=%async_computation.13 | async-start | bytes 1966080 | tf_op jit(solution)/shard_map/psum | solution.py:58
  59.7 130.1 %copy-start.8 = (f32[4,16,64]{2,1,0:T(8,128)S(1)}, f32[4,16,64]{2,1,0:T(8,128)}, u32[]{:S(2)}) copy-start(f32[4,16,64]{2,1,0:T(8,128)} %reduce_sum.228) | copy-start | bytes 49156
  60.7 196.6 %all-reduce.19.cloned.1.call-start = ((), (), s32[]{:S(2)}) async-start(), calls=%async_computation.15 | async-start | bytes 1966080 | tf_op jit(solution)/shard_map/psum | solution.py:58
  259.2 23.5 %all-to-all-start.5 = ((f32[8,4,1,16]{3,2,1,0:T(1,128)}), f32[8,4,1,16]{3,2,1,0:T(1,128)S(1)}, u32[]{:S(2)}, u32[]{:S(2)}) async-start(f32[8,4,1,16]{3,2,1,0:T(1,128)} %broadcast_in_dim.29), calls=%async_computation.5 | async-start | bytes 32768 | tf_op jit(solution)/shard_map/all_to_all | solution.py:14
  282.7 8.5 %all-to-all-start.9 = ((f32[8,1,128]{2,1,0:T(1,128)}), f32[8,1,128]{2,1,0:T(1,128)S(1)}, u32[]{:S(2)}, u32[]{:S(2)}) async-start(f32[8,1,128]{2,1,0:T(1,128)} %reshape.203), calls=%async_computation.9 | async-start | bytes 8192 | tf_op jit(solution)/shard_map/all_to_all | solution.py:14
  288.8 29.1 %copy-start.3 = (f32[4,2,16,512]{3,2,1,0:T(8,128)S(1)}, f32[4,2,16,512]{3,2,1,0:T(8,128)}, u32[]{:S(2)}) copy-start(f32[4,2,16,512]{3,2,1,0:T(8,128)} %get-tuple-element.27) | copy-start | bytes 786436
  291.1 0.6 copy-start.12
  291.7 11.3 %all-to-all-start.1 = ((f32[8,1,128]{2,1,0:T(1,128)}), f32[8,1,128]{2,1,0:T(1,128)S(1)}, u32[]{:S(2)}, u32[]{:S(2)}) async-start(f32[8,1,128]{2,1,0:T(1,128)} %reshape.193), calls=%async_computation.1 | async-start | bytes 8192 | tf_op jit(solution)/shard_map/all_to_all | solution.py:14
  303.0 10.2 %all-to-all-start.6 = ((f32[8,1,4096]{2,1,0:T(1,128)}), f32[8,1,4096]{2,1,0:T(1,128)}, u32[]{:S(2)}, u32[]{:S(2)}) async-start(f32[8,1,4096]{2,1,0:T(1,128)} %reshape.199), calls=%async_computation.6 | async-start | bytes 262144 | tf_op jit(solution)/shard_map/all_to_all | solution.py:14
  313.2 11.4 %all-to-all-start.10 = ((f32[8,1,8192]{2,1,0:T(1,128)}), f32[8,1,8192]{2,1,0:T(1,128)}, u32[]{:S(2)}, u32[]{:S(2)}) async-start(f32[8,1,8192]{2,1,0:T(1,128)} %reshape.205), calls=%async_computation.10 | async-start | bytes 524288 | tf_op jit(solution)/shard_map/all_to_all | solution.py:14
  326.6 20.2 %all-to-all-start.2 = ((f32[8,4,2,16,224]{4,3,2,1,0:T(8,128)}), f32[8,4,2,16,224]{4,3,2,1,0:T(8,128)}, u32[]{:S(2)}, u32[]{:S(2)}) async-start(f32[8,4,2,16,224]{4,3,2,1,0:T(8,128)} %broadcast_in_dim.26), calls=%async_computation.2 | async-start | bytes 2097152 | tf_op jit(solution)/shard_map/all_to_all | solution.py:14
  331.8 139.8 %all-reduce.13.cloned.1.call-start = ((), (), s32[]{:S(2)}) async-start(), calls=%async_computation.12 | async-start | bytes 1966080 | tf_op jit(solution)/shard_map/psum | solution.py:58
  348.2 123.4 %copy-start.9 = (f32[4,16,64]{2,1,0:T(8,128)S(1)}, f32[4,16,64]{2,1,0:T(8,128)}, u32[]{:S(2)}) copy-start(f32[4,16,64]{2,1,0:T(8,128)} %reduce_sum.233) | copy-start | bytes 49156
  349.3 189.7 %all-reduce.17.cloned.1.call-start = ((), (), s32[]{:S(2)}) async-start(), calls=%async_computation.14 | async-start | bytes 1966080 | tf_op jit(solution)/shard_map/psum | solution.py:58
  539.0 39.2 %copy-start.6 = (f32[4,2,16,512]{3,2,1,0:T(8,128)S(1)}, f32[4,2,16,512]{3,2,1,0:T(8,128)}, u32[]{:S(2)}) copy-start(f32[4,2,16,512]{3,2,1,0:T(8,128)} %get-tuple-element.26) | copy-start | bytes 786436
  539.0 43.8 %copy-start.5 = (f32[4,2,16,512]{3,2,1,0:T(8,128)S(1)}, f32[4,2,16,512]{3,2,1,0:T(8,128)}, u32[]{:S(2)}) copy-start(f32[4,2,16,512]{3,2,1,0:T(8,128)} %get-tuple-element.24) | copy-start | bytes 786436
  540.9 23.6 %all-to-all-start.7 = ((f32[8,4,1,16]{3,2,1,0:T(1,128)}), f32[8,4,1,16]{3,2,1,0:T(1,128)S(1)}, u32[]{:S(2)}, u32[]{:S(2)}) async-start(f32[8,4,1,16]{3,2,1,0:T(1,128)} %broadcast_in_dim.31), calls=%async_computation.7 | async-start | bytes 32768 | tf_op jit(solution)/shard_map/all_to_all | solution.py:14
  564.5 8.5 %all-to-all-start.11 = ((f32[8,1,128]{2,1,0:T(1,128)}), f32[8,1,128]{2,1,0:T(1,128)S(1)}, u32[]{:S(2)}, u32[]{:S(2)}) async-start(f32[8,1,128]{2,1,0:T(1,128)} %reshape.207), calls=%async_computation.11 | async-start | bytes 8192 | tf_op jit(solution)/shard_map/all_to_all | solution.py:14
  573.0 8.5 %all-to-all-start.3 = ((f32[8,1,128]{2,1,0:T(1,128)}), f32[8,1,128]{2,1,0:T(1,128)S(1)}, u32[]{:S(2)}, u32[]{:S(2)}) async-start(f32[8,1,128]{2,1,0:T(1,128)} %reshape.195), calls=%async_computation.3 | async-start | bytes 8192 | tf_op jit(solution)/shard_map/all_to_all | solution.py:14
Sparse Core Ops, SparseCore 0:
  60.9 128.8 all-reduce.14
  192.3 65.0 all-reduce.18
  349.4 122.0 all-reduce.12
  473.9 65.0 all-reduce.16
